TPU v7x, 32 devices: a whole 2x2x4 slice. The times are simulated.
32 devices in a mesh: grp: 2 (over y), vec: 4 (over z), walk: 2 (over x), orb: 2 (over core).
Axes of the slice: x: 2, y: 2, z: 4, core: 2. Of those that a mesh axis runs over, the one named last changes fastest.
Arguments:
- walkers: bfloat16 [32, 512, 128], P(('grp', 'walk'), 'orb'), parts along dimension 0, may hold values from -3 to 3
- inv_intersection: bfloat16 [32, 128, 128], P(('grp', 'walk')), parts along dimension 0, may hold values from -0.5 to 0.5
- trial: bfloat16 [512, 128], replicated, may hold values from -0.25 to 0.25
- vectors: bfloat16 [32, 512, 512], P('vec', 'orb')
- aux_field: float32 [32, 32], P(('grp', 'walk'), 'vec'), parts along dimension 0, may hold values from -5 to 5
- log_weight: float32 [32], P(('grp', 'walk')), parts along dimension 0, may hold values from -4 to 4
- copy_list: int32 [32], P(('grp', 'walk')), parts along dimension 0, may hold values from 0 to 15
Outputs:
- walkers_out: bfloat16 [32, 512, 128], P(('grp', 'walk'), 'orb'), parts along dimension 0
- weights_out: float32 [32], P(('grp', 'walk')), parts along dimension 0
There are 2 independent parts, one for each index of `grp`. A program takes and returns all parts, laid end to end along the dimension named above; an argument that names none is the same for every part. Nothing has to cross between parts.
Inputs may be any that keep to these rules, and one draw needn't show every extreme that they name: `copy_list`: the walker, within the same ensemble, whose copy fills the slot.
All inputs are finite; a program needn't handle non-finite values.
Results may differ from a plain program's by a relative error of at most 0.008.
Values may be sent and summed in bfloat16 or wider, within the bound.
A program may use at most 64 MiB of HBM per device.

v0:
```python
from functools import partial
import math

import jax
import jax.numpy as jnp
from jax import lax
from jax.sharding import PartitionSpec as P

ORDER = 6


step_root = math.sqrt(0.08)


def fold_rows(operator, carry, piece, start):
    return jnp.einsum("wnm,wme->wne", operator, piece, preferred_element_type=jnp.float32)


def per_device(walkers, inv_intersection, trial, vectors, aux_field, log_weight, copy_list):
    green = jnp.einsum(
        "wne,wef->wnf", walkers, inv_intersection, preferred_element_type=jnp.float32
    ).astype(jnp.bfloat16)
    mixed = jnp.einsum("gnm,me->gne", vectors, trial, preferred_element_type=jnp.float32).astype(
        jnp.bfloat16
    )
    partial_bias = jnp.einsum("wne,gne->wg", green, mixed, preferred_element_type=jnp.float32)
    bias = lax.psum(partial_bias, "orb")
    shift = -step_root * bias
    field = aux_field - shift
    own_factor = jnp.sum(aux_field * shift - 0.5 * shift * shift, axis=1)
    new_log = log_weight + lax.psum(own_factor, "vec")
    weighted = (field * step_root).astype(jnp.bfloat16)
    local_operator = jnp.einsum(
        "wg,gnm->wnm", weighted, vectors, preferred_element_type=jnp.float32
    )
    operator = lax.psum(local_operator, "vec").astype(jnp.bfloat16)
    running = walkers.astype(jnp.float32)
    folder = partial(fold_rows, operator)
    operand = walkers
    for degree in range(1, ORDER + 1):
        initial = jnp.zeros(running.shape, jnp.float32)
        summed = folder(initial, lax.all_gather(operand, "orb", axis=1, tiled=True), jnp.int32(0))
        new_term = (summed / degree).astype(jnp.bfloat16)
        running = running + new_term.astype(jnp.float32)
        if degree < ORDER:
            operand = new_term
    propagated = running.astype(jnp.bfloat16)
    every_walker = lax.all_gather(propagated, "walk", axis=0, tiled=True)
    every_log = lax.all_gather(new_log, "walk", axis=0, tiled=True)
    return (every_walker[copy_list], every_log[copy_list])


def solution(mesh):
    return jax.shard_map(
        per_device,
        mesh=mesh,
        in_specs=(
            P(("grp", "walk"), "orb", None),
            P(("grp", "walk"), None, None),
            P(),
            P("vec", "orb", None),
            P(("grp", "walk"), "vec"),
            P(("grp", "walk")),
            P(("grp", "walk")),
        ),
        out_specs=(P(("grp", "walk"), "orb", None), P(("grp", "walk"))),
        check_vma=False,
    )
```

profile of v0, /device:TPU:0, one launch (start us, length us, event | category | flops | bytes accessed | tf_op | source)
XLA Modules:
  0.0 276.8 jit_solution(15812537913773210420)
XLA Ops:
  7.2 0.0 copy-start
  7.2 0.0 copy-start.3
  7.2 0.0 all-gather.8.cloned.1.call-start
  7.2 0.7 all-gather.8.cloned.1.call-update
  7.9 0.0 all-gather.10.cloned.1.call-start
  8.0 1.4 convolution_convert_fusion.1
  9.4 0.4 copy.23
  9.8 0.0 copy-done
  9.8 0.0 copy-done.3
  9.8 0.0 copy-start.4
  9.8 1.5 convolution_convert_fusion.2
  11.3 1.4 copy.24
  12.7 0.4 convolution_bitcast_fusion
  13.2 2.6 psum.21
  15.8 0.0 copy-done.4
  15.8 3.3 %fusion = f32[8,256,512]{2,0,1:T(8,128)} fusion(bf16[8,256,512]{2,1,0:T(8,128)(2,1)S(1)} %copy-done, f32[8,8]{1,0:T(8,128)S(1)} %copy-done.4, f32[8,8]{1,0:T(8,128)S(1)} %psum.21), kind=kOutput, calls=%fused_computation.2 | convolution fusion | flops 16777472 | bytes 6291968 | tf_op jit(solution)/shard_map/wg,gnm->wnm/dot_general | solution.py:33
  19.1 0.1 subtract_reduce_fusion
  19.2 150.7 %all-reduce.3 = (bf16[8,256,512]{2,0,1:T(8,128)(2,1)}, f32[8]{0:T(128)S(1)}) all-reduce(f32[8,256,512]{2,0,1:T(8,128)} %fusion, f32[8]{0:T(128)S(1)} %subtract_reduce_fusion), channel_id=1, replica_groups=mesh['grp'=2,'vec'=4,'walk'=2,'orb'=2] {'vec'}, use_global_device_ids=true, to_apply=%region_1.0 | all-reduce | flops 1048584 | bytes 6291520 | tf_op jit(solution)/shard_map/psum | solution.py:36
  169.9 0.0 all-gather.8.cloned.1.call-done
  169.9 4.0 %convolution_convert_fusion = bf16[8,256,128]{2,1,0:T(8,128)(2,1)} fusion(bf16[8,512,128]{2,1,0:T(8,128)(2,1)} %all-gather.8.cloned.1.call-done, bf16[8,256,512]{2,0,1:T(8,128)(2,1)} %get-tuple-element.2), kind=kOutput, calls=%fused_computation.9 | convolution fusion | flops 268697600 | bytes 3670016 | tf_op jit(solution)/shard_map/wnm,wme->wne/dot_general | solution.py:16
  173.9 0.0 all-gather.10.cloned.1.call-update
  173.9 0.0 all-gather.12.cloned.1.call-start
  173.9 8.3 %all-gather.10.cloned.1.call-done = bf16[8,512,128]{2,1,0:T(8,128)(2,1)} async-done(((bf16[8,256,128]{2,1,0:T(8,128)(2,1)}), bf16[8,512,128]{2,1,0:T(8,128)(2,1)}) %all-gather.10.cloned.1.call-update) | async-done | bytes 1048592 | tf_op jit(solution)/shard_map/all_gather | solution.py:42
  182.2 4.1 %fusion.2 = bf16[8,256,128]{2,1,0:T(8,128)(2,1)} fusion(bf16[8,512,128]{2,1,0:T(8,128)(2,1)} %all-gather.10.cloned.1.call-done, bf16[8,256,512]{2,0,1:T(8,128)(2,1)} %get-tuple-element.2), kind=kOutput, calls=%fused_computation.11 | convolution fusion | flops 268959744 | bytes 3670016 | tf_op jit(solution)/shard_map/wnm,wme->wne/dot_general | solution.py:16
  186.3 0.0 all-gather.12.cloned.1.call-update
  186.3 0.0 all-gather.14.cloned.1.call-start
  186.4 10.3 %all-gather.12.cloned.1.call-done = bf16[8,512,128]{2,1,0:T(8,128)(2,1)} async-done(((bf16[8,256,128]{2,1,0:T(8,128)(2,1)}), bf16[8,512,128]{2,1,0:T(8,128)(2,1)}) %all-gather.12.cloned.1.call-update) | async-done | bytes 1048592 | tf_op jit(solution)/shard_map/all_gather | solution.py:42
  196.7 4.1 %fusion.3 = bf16[8,256,128]{2,1,0:T(8,128)(2,1)} fusion(bf16[8,512,128]{2,1,0:T(8,128)(2,1)} %all-gather.12.cloned.1.call-done, bf16[8,256,512]{2,0,1:T(8,128)(2,1)} %get-tuple-element.2), kind=kOutput, calls=%fused_computation.12 | convolution fusion | flops 268959744 | bytes 3670016 | tf_op jit(solution)/shard_map/wnm,wme->wne/dot_general | solution.py:16
  200.7 0.0 all-gather.14.cloned.1.call-update
  200.7 0.0 all-gather.16.cloned.1.call-start
  200.8 10.3 %all-gather.14.cloned.1.call-done = bf16[8,512,128]{2,1,0:T(8,128)(2,1)} async-done(((bf16[8,256,128]{2,1,0:T(8,128)(2,1)}), bf16[8,512,128]{2,1,0:T(8,128)(2,1)}) %all-gather.14.cloned.1.call-update) | async-done | bytes 1048592 | tf_op jit(solution)/shard_map/all_gather | solution.py:42
  211.1 4.0 %fusion.4 = bf16[8,256,128]{2,1,0:T(8,128)(2,1)} fusion(bf16[8,512,128]{2,1,0:T(8,128)(2,1)} %all-gather.14.cloned.1.call-done, bf16[8,256,512]{2,0,1:T(8,128)(2,1)} %get-tuple-element.2), kind=kOutput, calls=%fused_computation.13 | convolution fusion | flops 268959744 | bytes 3670016 | tf_op jit(solution)/shard_map/wnm,wme->wne/dot_general | solution.py:16
  215.1 0.0 all-gather.16.cloned.1.call-update
  215.2 0.0 copy-start.1
  215.2 0.0 copy-start.2
  215.2 0.0 all-gather.18.cloned.1.call-start
  215.2 10.3 %all-gather.16.cloned.1.call-done = bf16[8,512,128]{2,1,0:T(8,128)(2,1)} async-done(((bf16[8,256,128]{2,1,0:T(8,128)(2,1)}), bf16[8,512,128]{2,1,0:T(8,128)(2,1)}) %all-gather.16.cloned.1.call-update) | async-done | bytes 1048592 | tf_op jit(solution)/shard_map/all_gather | solution.py:42
  225.5 4.0 %fusion.5 = bf16[8,256,128]{2,1,0:T(8,128)(2,1)} fusion(bf16[8,512,128]{2,1,0:T(8,128)(2,1)} %all-gather.16.cloned.1.call-done, bf16[8,256,512]{2,0,1:T(8,128)(2,1)} %get-tuple-element.2), kind=kOutput, calls=%fused_computation.14 | convolution fusion | flops 268959744 | bytes 3670016 | tf_op jit(solution)/shard_map/wnm,wme->wne/dot_general | solution.py:16
  229.6 0.0 all-gather.18.cloned.1.call-update
  229.6 0.0 copy-start.7
  229.6 0.0 copy-start.5
  229.6 0.0 copy-start.6
  229.6 0.0 all-gather.20.cloned.1.call-start
  229.7 10.3 %all-gather.18.cloned.1.call-done = bf16[8,512,128]{2,1,0:T(8,128)(2,1)} async-done(((bf16[8,256,128]{2,1,0:T(8,128)(2,1)}), bf16[8,512,128]{2,1,0:T(8,128)(2,1)}) %all-gather.18.cloned.1.call-update) | async-done | bytes 1048592 | tf_op jit(solution)/shard_map/all_gather | solution.py:42
  239.9 0.0 copy-done.1
  239.9 0.0 copy-done.2
  239.9 4.7 %fusion.9 = bf16[8,256,128]{2,1,0:T(8,128)(2,1)} fusion(bf16[8,512,128]{2,1,0:T(8,128)(2,1)} %all-gather.18.cloned.1.call-done, bf16[8,256,128]{2,1,0:T(8,128)(2,1)} %fusion.5, bf16[8,256,128]{2,1,0:T(8,128)(2,1)} %fusion.4, bf16[8,256,128]{2,1,0:T(8,128)(2,1)} %fusion.3, bf16[8,256,128]{2,1,0:T(8,128)(2,1)} %fusion.2, ...), kind=kOutput, calls=%fused_computation.18 | convolution fusion | flops 272629760 | bytes 6815744 | tf_op jit(solution)/shard_map/wnm,wme->wne/dot_general | solution.py:16
  244.7 0.0 all-gather.20.cloned.1.call-update
  244.7 0.0 copy-done.7
  244.7 0.6 dynamic-slice
  246.0 0.0 copy-done.5
  246.0 0.1 add_dynamic-update-slice_fusion
  246.1 4.9 %all-reduce = f32[16]{0:T(128)S(1)} all-reduce(f32[16]{0:T(128)S(1)} %add_dynamic-update-slice_fusion), channel_id=1, replica_groups=mesh['grp'=2,'vec'=4,'walk'=2,'orb'=2] {'walk'}, use_global_device_ids=true, to_apply=%add | all-reduce | flops 16 | bytes 128
  251.0 0.0 copy-done.6
  251.0 1.2 gather_fusion.1
  252.2 15.2 %all-gather.20.cloned.1.call-done = bf16[16,256,128]{2,1,0:T(8,128)(2,1)} async-done(((bf16[8,256,128]{2,1,0:T(8,128)(2,1)}), bf16[16,256,128]{2,1,0:T(8,128)(2,1)}) %all-gather.20.cloned.1.call-update) | async-done | bytes 1048592 | tf_op jit(solution)/shard_map/all_gather | solution.py:48
  267.3 2.6 gather_fusion
  (3 shorter events, 0.0 us)
Async XLA Ops:
  7.2 2.6 copy-start
  7.2 2.6 copy-start.3
  7.2 162.7 %all-gather.8.cloned.1.call-start = ((), (), s32[]{:S(2)}) async-start(), calls=%async_computation | async-start | bytes 1572864 | tf_op jit(solution)/shard_map/all_gather | solution.py:42
  7.9 174.3 %all-gather.10.cloned.1.call-start = ((), (), s32[]{:S(2)}) async-start(), calls=%async_computation.1 | async-start | bytes 1572864 | tf_op jit(solution)/shard_map/all_gather | solution.py:42
  9.8 6.0 %copy-start.4 = (f32[8,8]{1,0:T(8,128)S(1)}, f32[8,8]{1,0:T(8,128)}, u32[]{:S(2)}) copy-start(f32[8,8]{1,0:T(8,128)} %param.11) | copy-start | bytes 772
  173.9 22.8 %all-gather.12.cloned.1.call-start = ((), (), s32[]{:S(2)}) async-start(), calls=%async_computation.2 | async-start | bytes 1572864 | tf_op jit(solution)/shard_map/all_gather | solution.py:42
  186.3 24.8 %all-gather.14.cloned.1.call-start = ((), (), s32[]{:S(2)}) async-start(), calls=%async_computation.3 | async-start | bytes 1572864 | tf_op jit(solution)/shard_map/all_gather | solution.py:42
  200.7 24.8 %all-gather.16.cloned.1.call-start = ((), (), s32[]{:S(2)}) async-start(), calls=%async_computation.4 | async-start | bytes 1572864 | tf_op jit(solution)/shard_map/all_gather | solution.py:42
  215.2 24.8 %copy-start.1 = (bf16[8,256,128]{2,1,0:T(8,128)(2,1)S(1)}, bf16[8,256,128]{2,1,0:T(8,128)(2,1)}, u32[]{:S(2)}) copy-start(bf16[8,256,128]{2,1,0:T(8,128)(2,1)} %param.7) | copy-start | bytes 1572868
  215.2 24.8 %copy-start.2 = (bf16[8,256,128]{2,1,0:T(8,128)(2,1)S(1)}, bf16[8,256,128]{2,1,0:T(8,128)(2,1)}, u32[]{:S(2)}) copy-start(bf16[8,256,128]{2,1,0:T(8,128)(2,1)} %convolution_convert_fusion) | copy-start | bytes 1572868
  215.2 24.8 %all-gather.18.cloned.1.call-start = ((), (), s32[]{:S(2)}) async-start(), calls=%async_computation.5 | async-start | bytes 1572864 | tf_op jit(solution)/shard_map/all_gather | solution.py:42
  229.6 15.1 %copy-start.7 = (u32[32]{0:T(128)S(1)}, u32[32]{0:T(128)}, u32[]{:S(2)}) copy-start(u32[32]{0:T(128)} %constant.31) | copy-start | bytes 388
  229.6 16.4 %copy-start.5 = (f32[8]{0:T(128)S(1)}, f32[8]{0:T(128)}, u32[]{:S(2)}) copy-start(f32[8]{0:T(128)} %param.12) | copy-start | bytes 100
  229.6 21.4 %copy-start.6 = (s32[8]{0:T(128)S(1)}, s32[8]{0:T(128)}, u32[]{:S(2)}) copy-start(s32[8]{0:T(128)} %param.13) | copy-start | bytes 100
  229.6 37.7 %all-gather.20.cloned.1.call-start = ((), (), s32[]{:S(2)}) async-start(), calls=%async_computation.6 | async-start | bytes 1572864 | tf_op jit(solution)/shard_map/all_gather | solution.py:48
Sparse Core Ops, SparseCore 0:
  9.5 11.7 all-gather.7
  174.0 8.1 all-gather.9
  186.4 10.1 all-gather.11
  200.9 10.1 all-gather.13
  215.3 10.1 all-gather.15
  229.7 10.1 all-gather.17
  244.8 22.4 all-gather.19
where the time goes:
time: 277 us
  blocking collectives  158 us (57%)
  waiting for transfers between devices  65.4 us (24%)
  matrix products  31.5 us (11%)
  between operations  14.9 us (5%)
  local copies, waits for them, and re-layouts  6.25 us (2%)
    psum x1, blocking collectives, per_device(): operator = lax.psum(local_operator, 'vec').astype(jnp.bfloat16)  151 us
    all_gather x6, waiting for transfers between devices, per_device(): lax.all_gather(operand, 'orb', axis=1, tiled=True)  49.4 us
    dot_general x6, matrix products, fold_rows(): jnp.einsum('wnm,wme->wne', operator, piece, preferred_element_type=jnp.fl...  24.9 us
    all_gather x1, waiting for transfers between devices, per_device(): every_walker = lax.all_gather(propagated, 'walk', axis=0, tiled=True)  15.2 us
  transfers between devices with their start and end apart: 7, of which 6 were waited for; matrix products, arithmetic and copies ran while one was open for 4% of the time, Pallas kernels for 0%

commit v1 on v0

v1 whole, which is shorter than its diff:
```python
import functools
import math

import jax
import jax.numpy as jnp
from jax import lax
from jax.experimental import pallas as pl
from jax.experimental.pallas import tpu as pltpu
from jax.sharding import PartitionSpec as P

ORDER = 6
PIECES = 2
MESH = pl.DeviceIdType.MESH
F32 = jnp.float32
BF16 = jnp.bfloat16

step_root = math.sqrt(0.08)


def remote(src, dst, send, recv, where):
    return pltpu.make_async_remote_copy(
        src_ref=src, dst_ref=dst, send_sem=send, recv_sem=recv, device_id=where, device_id_type=MESH
    )


def kernel(
    depth, width,
    walkers, inverse, trial, vectors, aux, log_weight, copy_list,
    out, out_log,
    green, mixed, bias_own, bias_in, other_rows, partial, arrived, leaving, operator, full, term, result, every,
    factor_in, factor_out, logs,
    bias_sems, rows_sems, chain_send, chain_recv, factor_send, factor_recv, swap_send, swap_recv,
    every_recv, own_sends, next_send, across_send, log_send, log_recv,
):
    z = lax.axis_index("vec")
    x = lax.axis_index("walk")
    o = lax.axis_index("orb")
    last = depth - 1
    local, rows, electrons = walkers.shape
    count, _, orbitals = vectors.shape
    half = local // 2
    block = orbitals // 4
    span = 2 * block // count
    wide = count * span
    packed = partial.shape[1]
    piece = packed // PIECES
    chunks = half * PIECES
    mine = half // 2

    barrier = pltpu.get_barrier_semaphore()

    def greet(where):
        pl.semaphore_signal(barrier, inc=1, device_id=where, device_id_type=MESH)

    greet({"orb": 1 - o})
    for hop in range(1, width):
        for core in range(2):
            greet({"walk": lax.rem(x + hop, width), "orb": core})

    @pl.when(z > 0)
    def _():
        for core in range(2):
            greet({"vec": z - 1, "orb": core})

    @pl.when(z < last)
    def _():
        for core in range(2):
            greet({"vec": z + 1, "orb": core})

    sides = jnp.where(z > 0, 2, 0) + jnp.where(z < last, 2, 0)
    pl.semaphore_wait(barrier, 1 + 2 * (width - 1) + sides)

    rows_copy = remote(walkers, other_rows, rows_sems.at[0], rows_sems.at[1], {"orb": 1 - o})
    rows_copy.start()

    for w in range(local):
        green[w] = jnp.dot(walkers[w], inverse[w], preferred_element_type=F32).astype(BF16)
    for g in range(count):
        mixed[g] = jnp.dot(vectors[g], trial[...], preferred_element_type=F32).astype(BF16)
    gram = jnp.zeros((local * span, wide), F32)
    for j in range(rows // span):
        left = green[:, j * span:(j + 1) * span, :].reshape(local * span, electrons)
        right = mixed[:, j * span:(j + 1) * span, :].reshape(wide, electrons)
        gram = gram + lax.dot_general(left, right, (((1,), (1,)), ((), ())), preferred_element_type=F32)
    row_id = lax.broadcasted_iota(jnp.int32, (local * span, wide), 0)
    col_id = lax.broadcasted_iota(jnp.int32, (local * span, wide), 1)
    same = row_id % span == col_id % span
    folded = jnp.sum(jnp.where(same, gram, 0.0).reshape(local, span, wide), axis=1)
    wide_row = lax.broadcasted_iota(jnp.int32, (wide, wide), 0)
    wide_col = lax.broadcasted_iota(jnp.int32, (wide, wide), 1)
    groups = jnp.where(wide_row // span == wide_col // span, 1.0, 0.0).astype(F32)
    bias_own[...] = jnp.dot(folded, groups, precision=lax.Precision.HIGHEST, preferred_element_type=F32)
    bias_copy = remote(bias_own, bias_in, bias_sems.at[0], bias_sems.at[1], {"orb": 1 - o})
    bias_copy.start()
    bias_copy.wait()
    bias = bias_own[...] + bias_in[...]
    shift = -step_root * bias
    field = aux[...] - shift
    factor = jnp.sum(aux[...] * shift - 0.5 * shift * shift, axis=1, keepdims=True) * (1.0 / span)
    factor = jnp.broadcast_to(factor, (local, logs.shape[2]))
    weighted = (field * step_root).astype(BF16).astype(F32)
    spread = jnp.broadcast_to(weighted[:, None, :], (local, span, wide)).reshape(local * span, wide)
    kron = jnp.where(same, spread, 0.0).astype(BF16)

    for j in range(block // span):
        here = slice(j * span, (j + 1) * span)
        cols = pl.ds(pl.multiple_of(o * block, block), 3 * block)
        strip = vectors[:, here, cols].reshape(wide, 3 * block)
        summed = jnp.dot(kron, strip, preferred_element_type=F32)
        for slot in range(3):
            partial[:, slot * block + j * span:slot * block + (j + 1) * span, :] = summed[
                :, slot * block:(slot + 1) * block
            ].reshape(local, span, block)
        below = slice(block + j * span, block + (j + 1) * span)
        one = vectors[:, below, pl.ds(pl.multiple_of((1 - o) * block, block), block)].reshape(wide, block)
        two = vectors[:, below, 3 * block:].reshape(wide, block)
        summed = jnp.dot(kron, jnp.concatenate([one, two], axis=1), preferred_element_type=F32)
        for slot in range(2):
            partial[:, (3 + slot) * block + j * span:(3 + slot) * block + (j + 1) * span, :] = summed[
                :, slot * block:(slot + 1) * block
            ].reshape(local, span, block)

    to_next = [z - 1, z + 1]
    upstream = [last - z, z]
    downstream = [z, last - z]

    def chain_copy(side, c):
        return remote(
            leaving.at[side, c], arrived.at[side, c], chain_send.at[side, c], chain_recv.at[side, c],
            {"vec": to_next[side]},
        )

    def factor_copy(side):
        return remote(
            factor_out.at[side], factor_in.at[side], factor_send.at[side], factor_recv.at[side],
            {"vec": to_next[side]},
        )

    def swap_copy(c):
        return remote(operator.at[o, c], operator.at[o, c], swap_send.at[c], swap_recv.at[c], {"orb": 1 - o})

    def swap_arrival(c):
        return remote(operator.at[1 - o, c], operator.at[1 - o, c], swap_send.at[c], swap_recv.at[c], {"orb": 1 - o})

    def chain_step(t, carry):
        for side in range(2):
            c = t - upstream[side]
            head = upstream[side] == 0
            owner = downstream[side] == 0

            @pl.when((c >= 0) & (c < chunks))
            def _():
                own = partial[side * half + c // PIECES, pl.ds(pl.multiple_of((c % PIECES) * piece, piece), piece), :]

                @pl.when(head)
                def _():
                    leaving[side, c] = own.astype(BF16)

                @pl.when(jnp.logical_not(head))
                def _():
                    chain_copy(side, c).wait_recv()
                    both = (own + arrived[side, c].astype(F32)).astype(BF16)

                    @pl.when(owner)
                    def _():
                        operator[o, c] = both

                    @pl.when(jnp.logical_not(owner))
                    def _():
                        leaving[side, c] = both

                @pl.when(jnp.logical_not(owner))
                def _():
                    chain_copy(side, c).start()

                @pl.when(owner & ((c // PIECES) % 2 != o))
                def _():
                    swap_copy(c).start()

                @pl.when(c == 0)
                def _():
                    @pl.when(head)
                    def _():
                        factor_in[side] = jnp.zeros_like(factor)

                    @pl.when(jnp.logical_not(head))
                    def _():
                        factor_copy(side).wait_recv()

                    @pl.when(jnp.logical_not(owner))
                    def _():
                        factor_out[side] = factor_in[side] + factor
                        factor_copy(side).start()

        return carry

    lax.fori_loop(0, chunks + last, chain_step, jnp.int32(0))

    def log_copy(hop):
        other = lax.rem(x + hop, width)
        return remote(logs.at[x], logs.at[x], log_send.at[hop - 1], log_recv.at[x], {"walk": other})

    logs[x] = log_weight[...] + factor + factor_in[0] + factor_in[1]
    for hop in range(1, width):
        log_copy(hop).start()

    at_end = (z == 0) | (z == last)
    base = jnp.where(z == 0, 0, half)
    inward = jnp.where(z == 0, 1, last - 1)
    rows_copy.wait_recv()

    def place(w):
        return every.at[x * local + w]

    def own_copies(i):
        w = base + 2 * i + o
        copies = []
        for core in range(2):
            copies.append((core, {"vec": inward, "orb": core}))
        for hop in range(1, width):
            for core in range(2):
                copies.append((core, {"walk": lax.rem(x + hop, width), "orb": core}))
        made = [
            remote(result.at[i, core], place(w), own_sends.at[i, n], every_recv.at[x, w], where)
            for n, (core, where) in enumerate(copies)
        ]
        made.append(
            remote(result.at[i, 1 - o], place(w), own_sends.at[i, len(copies)], every_recv.at[x, w], {"orb": 1 - o})
        )
        return made

    @pl.when(at_end)
    def _():
        for i in range(mine):
            a = 2 * i + o
            w = base + a
            for q in range(PIECES):
                swap_arrival(a * PIECES + q).wait_recv()

            def tile(core, slot):
                flat = operator[core, pl.ds(a * PIECES, PIECES)].reshape(packed, block)
                return flat[slot * block:(slot + 1) * block, :]

            def put(r, c, value):
                full[r * block:(r + 1) * block, c * block:(c + 1) * block] = value

            spots = (((0, 0), (0, 1), (0, 2), (1, 1), (1, 3)), ((2, 1), (2, 2), (2, 3), (3, 0), (3, 3)))
            for core in range(2):
                for slot in range(5):
                    r, c = spots[core][slot]
                    value = tile(core, slot)
                    put(r, c, value)
                    if r != c:
                        put(c, r, value.T)
            term[pl.ds(pl.multiple_of(o * rows, rows), rows), :] = walkers[w]
            term[pl.ds(pl.multiple_of((1 - o) * rows, rows), rows), :] = other_rows[w]
            running = term[...].astype(F32)
            for degree in range(1, ORDER + 1):
                fresh = (jnp.dot(full[...], term[...], preferred_element_type=F32) * (1.0 / degree)).astype(BF16)
                running = running + fresh.astype(F32)
                if degree < ORDER:
                    term[...] = fresh
            result[i] = running.astype(BF16).reshape(2, rows, electrons)
            for copy in own_copies(i):
                copy.start()
            every[x * local + w] = result[i, o]

    def onward(side, w, hop_to):
        return remote(place(w), place(w), next_send.at[w], every_recv.at[x, w], {"vec": hop_to})

    def across(w, hop):
        return remote(
            place(w), place(w), across_send.at[hop - 1, w], every_recv.at[x, w], {"walk": lax.rem(x + hop, width)}
        )

    for a in range(half):
        for side in range(2):
            w = side * half + a
            away = [z, last - z][side]
            hop_to = [z + 1, z - 1][side]
            end = [last - z, z][side]

            @pl.when(away > 0)
            def _():
                onward(side, w, hop_to).wait_recv()

                @pl.when(end > 0)
                def _():
                    onward(side, w, hop_to).start()

                for hop in range(1, width):
                    across(w, hop).start()

            if True:
                @pl.when((away == 0) & (o != a % 2))
                def _():
                    onward(side, w, hop_to).wait_recv()

    for hop in range(1, width):
        other = lax.rem(x + hop, width)
        for w in range(local):
            spot = every.at[other * local + w]
            remote(spot, spot, across_send.at[hop - 1, w], every_recv.at[other, w], {"walk": other}).wait_recv()
        remote(logs.at[other], logs.at[other], log_send.at[hop - 1], log_recv.at[other], {"walk": other}).wait_recv()

    for s in range(local):
        source = copy_list[s]
        out[s] = every[source]
        out_log[pl.ds(s, 1), :] = logs[source // local, pl.ds(source % local, 1), :]

    rows_copy.wait_send()
    for hop in range(1, width):
        log_copy(hop).wait_send()

    def drain(c, carry):
        for side in range(2):
            @pl.when(downstream[side] > 0)
            def _():
                chain_copy(side, c).wait_send()

        @pl.when(at_end & ((c // PIECES) % 2 != o))
        def _():
            swap_copy(c).wait_send()

        return carry

    lax.fori_loop(0, chunks, drain, jnp.int32(0))
    for side in range(2):
        @pl.when(downstream[side] > 0)
        def _():
            factor_copy(side).wait_send()

    @pl.when(at_end)
    def _():
        for i in range(mine):
            for copy in own_copies(i):
                copy.wait_send()

    for a in range(half):
        for side in range(2):
            w = side * half + a
            away = [z, last - z][side]
            hop_to = [z + 1, z - 1][side]
            end = [last - z, z][side]

            @pl.when(away > 0)
            def _():
                @pl.when(end > 0)
                def _():
                    onward(side, w, hop_to).wait_send()

                for hop in range(1, width):
                    across(w, hop).wait_send()


def per_device(depth, width, walkers, inv_intersection, trial, vectors, aux_field, log_weight, copy_list):
    local, rows, electrons = walkers.shape
    count, _, orbitals = vectors.shape
    half = local // 2
    block = orbitals // 4
    span = 2 * block // count
    wide = count * span
    packed = 5 * block
    piece = packed // PIECES
    chunks = half * PIECES
    mine = half // 2
    lanes = 128
    aux = jnp.repeat(aux_field, span, axis=1)
    log_wide = jnp.broadcast_to(log_weight[:, None], (local, lanes))
    vmem = pl.BlockSpec(memory_space=pltpu.VMEM)
    dma = pltpu.SemaphoreType.DMA
    out, out_log = pl.pallas_call(
        functools.partial(kernel, depth, width),
        out_shape=(
            jax.ShapeDtypeStruct(walkers.shape, BF16),
            jax.ShapeDtypeStruct((local, lanes), F32),
        ),
        in_specs=[vmem] * 6 + [pl.BlockSpec(memory_space=pltpu.SMEM)],
        out_specs=(vmem, vmem),
        scratch_shapes=[
            pltpu.VMEM((local, rows, electrons), BF16),
            pltpu.VMEM((count, rows, electrons), BF16),
            pltpu.VMEM((local, wide), F32),
            pltpu.VMEM((local, wide), F32),
            pltpu.VMEM((local, rows, electrons), BF16),
            pltpu.VMEM((local, packed, block), F32),
            pltpu.VMEM((2, chunks, piece, block), BF16),
            pltpu.VMEM((2, chunks, piece, block), BF16),
            pltpu.VMEM((2, chunks, piece, block), BF16),
            pltpu.VMEM((orbitals, orbitals), BF16),
            pltpu.VMEM((orbitals, electrons), BF16),
            pltpu.VMEM((mine, 2, rows, electrons), BF16),
            pltpu.VMEM((width * local, rows, electrons), BF16),
            pltpu.VMEM((2, local, lanes), F32),
            pltpu.VMEM((2, local, lanes), F32),
            pltpu.VMEM((width, local, lanes), F32),
            dma((2,)),
            dma((2,)),
            dma((2, chunks)),
            dma((2, chunks)),
            dma((2,)),
            dma((2,)),
            dma((chunks,)),
            dma((chunks,)),
            dma((width, local)),
            dma((mine, 2 * width + 1)),
            dma((local,)),
            dma((max(width - 1, 1), local)),
            dma((max(width - 1, 1),)),
            dma((width,)),
        ],
        compiler_params=pltpu.CompilerParams(collective_id=0, has_side_effects=True),
    )(walkers, inv_intersection, trial, vectors, aux, log_wide, copy_list)
    return out, out_log[:, 0]


def solution(mesh):
    depth, width = mesh.shape["vec"], mesh.shape["walk"]
    assert mesh.shape["orb"] == 2 and depth > 1
    return jax.shard_map(
        functools.partial(per_device, depth, width),
        mesh=mesh,
        in_specs=(
            P(("grp", "walk"), "orb", None),
            P(("grp", "walk"), None, None),
            P(),
            P("vec", "orb", None),
            P(("grp", "walk"), "vec"),
            P(("grp", "walk")),
            P(("grp", "walk")),
        ),
        out_specs=(P(("grp", "walk"), "orb", None), P(("grp", "walk"))),
        check_vma=False,
    )
```

time: 277 us -> 91.6 us (0.33)
  blocking collectives: 158 us -> 0 us
  Pallas kernels: 0 us -> 84.8 us
  waiting for transfers between devices: 65.4 us -> 0 us
  matrix products: 31.5 us -> 0 us
  between operations: 14.9 us -> 0.64 us
    psum x2 -> x0, blocking collectives: 153 us -> none  [the longest x1 151 us: per_device(): operator = lax.psum(local_operator, 'vec').astype(jnp.bfloat16)]
    pallas_call x0 -> x1, Pallas kernels: none -> 84.8 us  [per_device(): pl.pallas_call(functools.partial(kernel, depth, width), out_shape=(jax.Sh...]
    all_gather x7 -> x0, waiting for transfers between devices: 64.6 us -> none  [the longest x6 49.4 us: per_device(): lax.all_gather(operand, 'orb', axis=1, tiled=True)]
    dot_general x10 -> x0, matrix products: 31.5 us -> none  [the longest x6 24.9 us: fold_rows(): jnp.einsum('wnm,wme->wne', operator, piece, preferred_element_type=jnp.fl...]
    unnamed x1 -> x0, blocking collectives: 4.91 us -> none
    gather x2 -> x0, local copies, waits for them, and re-layouts: 3.78 us -> none  [per_device(): return (every_walker[copy_list], every_log[copy_list])]
  transfers between devices with their start and end apart: 7 -> 0, of which waited for: 6 -> 0; matrix products, arithmetic and copies ran while one was open for 4% -> 0% of each run, Pallas kernels for 0% -> 0%
where the time goes in v1:
time: 91.6 us; the launch traced here: 91.3 us
  Pallas kernels  84.8 us (93%)
  local copies, waits for them, and re-layouts  5.92 us (6%)
    pallas_call x1, Pallas kernels, per_device(): pl.pallas_call(functools.partial(kernel, depth, width), out_shape=(jax.Sh...  84.8 us
    unnamed x1, local copies, waits for them, and re-layouts  1.87 us

profile of v1, /device:TPU:0, one launch (start us, length us, event | category | flops | bytes accessed | tf_op | source)
XLA Modules:
  0.0 91.3 jit_solution(2681433742535298809)
XLA Ops:
  0.6 1.3 %broadcast_in_dim.10.log_weight = f32[8,128]{1,0:T(8,128)} broadcast(f32[8]{0:T(128)} %param.12), dimensions={0} | broadcast | bytes 4128 | tf_op jit(solution)/shard_map/broadcast_in_dim | solution.py:369
  1.9 0.8 broadcast_in_dim.4
  2.7 0.7 reshape.8.aux
  3.4 84.8 %shard_map.86 = (bf16[8,256,128]{2,1,0:T(8,128)(2,1)}, f32[8,128]{1,0:T(8,128)}) custom-call(bf16[8,256,128]{2,1,0:T(8,128)(2,1)} %walkers.1, bf16[8,128,128]{2,1,0:T(8,128)(2,1)} %inverse.1, bf16[512,128]{1,0:T(8,128)(2,1)} %trial.1, bf16[8,256,512]{2,1,0:T(8,128)(2,1)} %vectors.1, f32[8,256]{1,0:T(8,128)} %reshape.8.aux, ...), custom_call_target="tpu_custom_call" | custom-call | tf_op jit(solution)/shard_map/pallas_call | solution.py:372
  88.1 1.3 %slice_reduce_fusion = f32[8]{0:T(128)} fusion(f32[8,128]{1,0:T(8,128)} %get-tuple-element.5), kind=kLoop, calls=%fused_computation | loop fusion | bytes 64 | tf_op jit(solution)/shard_map/slice | solution.py:414
  89.4 1.9 %copy.10 = bf16[8,256,128]{2,1,0:T(8,128)(2,1)} copy(bf16[8,256,128]{2,1,0:T(8,128)(2,1)} %get-tuple-element.8) | data formatting | bytes 1048576

commit v2 on v1

--- a/solution.py
+++ b/solution.py
@@ -9,7 +9,8 @@
 from jax.sharding import PartitionSpec as P
 
 ORDER = 6
-PIECES = 2
+PIECES = 4
+SKEW = 4
 MESH = pl.DeviceIdType.MESH
 F32 = jnp.float32
 BF16 = jnp.bfloat16
@@ -90,13 +91,17 @@
     wide_col = lax.broadcasted_iota(jnp.int32, (wide, wide), 1)
     groups = jnp.where(wide_row // span == wide_col // span, 1.0, 0.0).astype(F32)
     bias_own[...] = jnp.dot(folded, groups, precision=lax.Precision.HIGHEST, preferred_element_type=F32)
+    pick_row = lax.broadcasted_iota(jnp.int32, (count, wide), 0)
+    pick_col = lax.broadcasted_iota(jnp.int32, (count, wide), 1)
+    pick = jnp.where(pick_row == pick_col // span, 1.0, 0.0).astype(F32)
+    drawn = jnp.dot(aux[...], pick, precision=lax.Precision.HIGHEST, preferred_element_type=F32)
     bias_copy = remote(bias_own, bias_in, bias_sems.at[0], bias_sems.at[1], {"orb": 1 - o})
     bias_copy.start()
     bias_copy.wait()
     bias = bias_own[...] + bias_in[...]
     shift = -step_root * bias
-    field = aux[...] - shift
-    factor = jnp.sum(aux[...] * shift - 0.5 * shift * shift, axis=1, keepdims=True) * (1.0 / span)
+    field = drawn - shift
+    factor = jnp.sum(drawn * shift - 0.5 * shift * shift, axis=1, keepdims=True) * (1.0 / span)
     factor = jnp.broadcast_to(factor, (local, logs.shape[2]))
     weighted = (field * step_root).astype(BF16).astype(F32)
     spread = jnp.broadcast_to(weighted[:, None, :], (local, span, wide)).reshape(local * span, wide)
@@ -144,7 +149,7 @@
 
     def chain_step(t, carry):
         for side in range(2):
-            c = t - upstream[side]
+            c = t - SKEW * upstream[side]
             head = upstream[side] == 0
             owner = downstream[side] == 0
 
@@ -193,16 +198,6 @@
                         factor_copy(side).start()
 
         return carry
-
-    lax.fori_loop(0, chunks + last, chain_step, jnp.int32(0))
-
-    def log_copy(hop):
-        other = lax.rem(x + hop, width)
-        return remote(logs.at[x], logs.at[x], log_send.at[hop - 1], log_recv.at[x], {"walk": other})
-
-    logs[x] = log_weight[...] + factor + factor_in[0] + factor_in[1]
-    for hop in range(1, width):
-        log_copy(hop).start()
 
     at_end = (z == 0) | (z == last)
     base = jnp.where(z == 0, 0, half)
@@ -229,9 +224,9 @@
         )
         return made
 
-    @pl.when(at_end)
-    def _():
-        for i in range(mine):
+    def finish(i):
+        @pl.when(at_end)
+        def _():
             a = 2 * i + o
             w = base + a
             for q in range(PIECES):
@@ -265,7 +260,27 @@
                 copy.start()
             every[x * local + w] = result[i, o]
 
-    def onward(side, w, hop_to):
+    begun = 0
+    for i in range(mine):
+        until = SKEW * last + (2 * i + 2) * PIECES
+        lax.fori_loop(begun, until, chain_step, jnp.int32(0))
+        begun = until
+        finish(i)
+
+
+    def log_copy(hop):
+        other = lax.rem(x + hop, width)
+        return remote(logs.at[x], logs.at[x], log_send.at[hop - 1], log_recv.at[x], {"walk": other})
+
+    walker_id = lax.broadcasted_iota(jnp.int32, factor.shape, 0)
+    weights = jnp.zeros(factor.shape, F32)
+    for w in range(local):
+        weights = jnp.where(walker_id == w, log_weight[w], weights)
+    logs[x] = weights + factor + factor_in[0] + factor_in[1]
+    for hop in range(1, width):
+        log_copy(hop).start()
+
+    def onward(w, hop_to):
         return remote(place(w), place(w), next_send.at[w], every_recv.at[x, w], {"vec": hop_to})
 
     def across(w, hop):
@@ -273,28 +288,33 @@
             place(w), place(w), across_send.at[hop - 1, w], every_recv.at[x, w], {"walk": lax.rem(x + hop, width)}
         )
 
-    for a in range(half):
-        for side in range(2):
-            w = side * half + a
-            away = [z, last - z][side]
-            hop_to = [z + 1, z - 1][side]
-            end = [last - z, z][side]
-
-            @pl.when(away > 0)
-            def _():
-                onward(side, w, hop_to).wait_recv()
-
-                @pl.when(end > 0)
-                def _():
-                    onward(side, w, hop_to).start()
-
-                for hop in range(1, width):
-                    across(w, hop).start()
-
-            if True:
+    near = jnp.where(z <= last - z, 0, 1)
+
+    def route(side, a):
+        w = side * half + a
+        away = jnp.where(side == 0, z, last - z)
+        hop_to = jnp.where(side == 0, z + 1, z - 1)
+        return w, away, last - away, hop_to
+
+    for i in range(mine):
+        for side in (near, 1 - near):
+            for a in (2 * i, 2 * i + 1):
+                w, away, end, hop_to = route(side, a)
+
+                @pl.when(away > 0)
+                def _():
+                    onward(w, hop_to).wait_recv()
+
+                    @pl.when(end > 0)
+                    def _():
+                        onward(w, hop_to).start()
+
+                    for hop in range(1, width):
+                        across(w, hop).start()
+
                 @pl.when((away == 0) & (o != a % 2))
                 def _():
-                    onward(side, w, hop_to).wait_recv()
+                    onward(w, hop_to).wait_recv()
 
     for hop in range(1, width):
         other = lax.rem(x + hop, width)
@@ -306,7 +326,7 @@
     for s in range(local):
         source = copy_list[s]
         out[s] = every[source]
-        out_log[pl.ds(s, 1), :] = logs[source // local, pl.ds(source % local, 1), :]
+        out_log[s] = jnp.max(logs[source // local, pl.ds(source % local, 1), :])
 
     rows_copy.wait_send()
     for hop in range(1, width):
@@ -339,15 +359,13 @@
     for a in range(half):
         for side in range(2):
             w = side * half + a
-            away = [z, last - z][side]
-            hop_to = [z + 1, z - 1][side]
-            end = [last - z, z][side]
+            _, away, end, hop_to = route(side, a)
 
             @pl.when(away > 0)
             def _():
                 @pl.when(end > 0)
                 def _():
-                    onward(side, w, hop_to).wait_send()
+                    onward(w, hop_to).wait_send()
 
                 for hop in range(1, width):
                     across(w, hop).wait_send()
@@ -365,18 +383,17 @@
     chunks = half * PIECES
     mine = half // 2
     lanes = 128
-    aux = jnp.repeat(aux_field, span, axis=1)
-    log_wide = jnp.broadcast_to(log_weight[:, None], (local, lanes))
     vmem = pl.BlockSpec(memory_space=pltpu.VMEM)
+    smem = pl.BlockSpec(memory_space=pltpu.SMEM)
     dma = pltpu.SemaphoreType.DMA
     out, out_log = pl.pallas_call(
         functools.partial(kernel, depth, width),
         out_shape=(
             jax.ShapeDtypeStruct(walkers.shape, BF16),
-            jax.ShapeDtypeStruct((local, lanes), F32),
+            jax.ShapeDtypeStruct((local,), F32),
         ),
-        in_specs=[vmem] * 6 + [pl.BlockSpec(memory_space=pltpu.SMEM)],
-        out_specs=(vmem, vmem),
+        in_specs=[vmem] * 5 + [smem] * 2,
+        out_specs=(vmem, smem),
         scratch_shapes=[
             pltpu.VMEM((local, rows, electrons), BF16),
             pltpu.VMEM((count, rows, electrons), BF16),
@@ -410,8 +427,8 @@
             dma((width,)),
         ],
         compiler_params=pltpu.CompilerParams(collective_id=0, has_side_effects=True),
-    )(walkers, inv_intersection, trial, vectors, aux, log_wide, copy_list)
-    return out, out_log[:, 0]
+    )(walkers, inv_intersection, trial, vectors, aux_field, log_weight, copy_list)
+    return out, out_log
 
 
 def solution(mesh):

time: 91.6 us -> 56.4 us (0.62)
  Pallas kernels: 84.8 us -> 52.6 us
  local copies, waits for them, and re-layouts: 5.92 us -> 2.98 us
    pallas_call x1, Pallas kernels: 84.8 us -> 52.6 us  [per_device(): pl.pallas_call(functools.partial(kernel, depth, width), out_shape=(jax.Sh...]
    broadcast_in_dim x2 -> x0, local copies, waits for them, and re-layouts: 2.07 us -> none  [the longest x1 1.32 us: per_device(): log_wide = jnp.broadcast_to(log_weight[:, None], (local, lanes))]
    slice x1 -> x0, local copies, waits for them, and re-layouts: 1.3 us -> none  [per_device(): return (out, out_log[:, 0])]
    unnamed x1 -> x2, local copies, waits for them, and re-layouts: 1.87 us -> 2.98 us
where the time goes in v2:
time: 56.4 us; the launch traced here: 56.2 us
  Pallas kernels  52.6 us (93%)
  local copies, waits for them, and re-layouts  2.98 us (5%)
  between operations  0.64 us (1%)
    pallas_call x1, Pallas kernels, per_device(): pl.pallas_call(functools.partial(kernel, depth, width), out_shape=(jax.Sh...  52.6 us
    unnamed x2, local copies, waits for them, and re-layouts  2.98 us

profile of v2, /device:TPU:0, one launch (start us, length us, event | category | flops | bytes accessed | tf_op | source)
XLA Modules:
  0.0 56.2 jit_solution(8785135172128541098)
XLA Ops:
  0.6 52.6 %shard_map.86 = (bf16[8,256,128]{2,1,0:T(8,128)(2,1)}, f32[8]{0:T(128)}) custom-call(bf16[8,256,128]{2,1,0:T(8,128)(2,1)} %walkers.1, bf16[8,128,128]{2,1,0:T(8,128)(2,1)} %inverse.1, bf16[512,128]{1,0:T(8,128)(2,1)} %trial.1, bf16[8,256,512]{2,1,0:T(8,128)(2,1)} %vectors.1, f32[8,8]{1,0:T(8,128)} %aux.1, f32[8]{0:T(128)} %log_weight.1, s32[8]{0:T(128)} %copy_list.1), custom_call_target="tpu_custom_call" | custom-call | tf_op jit(solution)/shard_map/pallas_call | solution.py:389
  53.2 1.9 %copy.11 = bf16[8,256,128]{2,1,0:T(8,128)(2,1)} copy(bf16[8,256,128]{2,1,0:T(8,128)(2,1)} %get-tuple-element.4) | data formatting | bytes 1048576
  55.1 1.1 %copy.12 = f32[8]{0:T(128)} copy(f32[8]{0:T(128)} %get-tuple-element.5) | data formatting | bytes 64

commit v3 on v2

--- a/solution.py
+++ b/solution.py
@@ -11,6 +11,7 @@
 ORDER = 6
 PIECES = 4
 SKEW = 4
+PARTS = 2
 MESH = pl.DeviceIdType.MESH
 F32 = jnp.float32
 BF16 = jnp.bfloat16
@@ -28,9 +29,9 @@
     depth, width,
     walkers, inverse, trial, vectors, aux, log_weight, copy_list,
     out, out_log,
-    green, mixed, bias_own, bias_in, other_rows, partial, arrived, leaving, operator, full, term, result, every,
+    green, mixed, bias_own, bias_in, other_rows, partial, arrived, leaving, crossed, given, operator, full, term, result, every,
     factor_in, factor_out, logs,
-    bias_sems, rows_sems, chain_send, chain_recv, factor_send, factor_recv, swap_send, swap_recv,
+    bias_sems, rows_sems, chain_send, chain_recv, factor_send, factor_recv, swap_send, swap_recv, cross_recv,
     every_recv, own_sends, next_send, across_send, log_send, log_recv,
 ):
     z = lax.axis_index("vec")
@@ -67,12 +68,6 @@
     def _():
         for core in range(2):
             greet({"vec": z + 1, "orb": core})
-
-    sides = jnp.where(z > 0, 2, 0) + jnp.where(z < last, 2, 0)
-    pl.semaphore_wait(barrier, 1 + 2 * (width - 1) + sides)
-
-    rows_copy = remote(walkers, other_rows, rows_sems.at[0], rows_sems.at[1], {"orb": 1 - o})
-    rows_copy.start()
 
     for w in range(local):
         green[w] = jnp.dot(walkers[w], inverse[w], preferred_element_type=F32).astype(BF16)
@@ -95,6 +90,12 @@
     pick_col = lax.broadcasted_iota(jnp.int32, (count, wide), 1)
     pick = jnp.where(pick_row == pick_col // span, 1.0, 0.0).astype(F32)
     drawn = jnp.dot(aux[...], pick, precision=lax.Precision.HIGHEST, preferred_element_type=F32)
+    sides = jnp.where(z > 0, 2, 0) + jnp.where(z < last, 2, 0)
+    pl.semaphore_wait(barrier, 1 + 2 * (width - 1) + sides)
+
+    rows_copy = remote(walkers, other_rows, rows_sems.at[0], rows_sems.at[1], {"orb": 1 - o})
+    rows_copy.start()
+
     bias_copy = remote(bias_own, bias_in, bias_sems.at[0], bias_sems.at[1], {"orb": 1 - o})
     bias_copy.start()
     bias_copy.wait()
@@ -141,11 +142,29 @@
             {"vec": to_next[side]},
         )
 
+    def cross_copy(side, c):
+        return remote(
+            leaving.at[side, c], crossed.at[c], chain_send.at[side, c], cross_recv.at[c],
+            {"vec": to_next[side], "orb": 1 - o},
+        )
+
+    end_side = jnp.where(z == 0, 0, 1)
+
     def swap_copy(c):
-        return remote(operator.at[o, c], operator.at[o, c], swap_send.at[c], swap_recv.at[c], {"orb": 1 - o})
-
-    def swap_arrival(c):
-        return remote(operator.at[1 - o, c], operator.at[1 - o, c], swap_send.at[c], swap_recv.at[c], {"orb": 1 - o})
+        return remote(leaving.at[end_side, c], given.at[c], swap_send.at[c], swap_recv.at[c], {"orb": 1 - o})
+
+    def part_of(side, c):
+        return partial[side * half + c // PIECES, pl.ds(pl.multiple_of((c % PIECES) * piece, piece), piece), :]
+
+    def give(c, carry):
+        @pl.when(((z == 0) | (z == last)) & ((c // PIECES) % 2 != o))
+        def _():
+            leaving[end_side, c] = part_of(end_side, c).astype(BF16)
+            swap_copy(c).start()
+
+        return carry
+
+    lax.fori_loop(0, chunks, give, jnp.int32(0))
 
     def chain_step(t, carry):
         for side in range(2):
@@ -155,32 +174,33 @@
 
             @pl.when((c >= 0) & (c < chunks))
             def _():
-                own = partial[side * half + c // PIECES, pl.ds(pl.multiple_of((c % PIECES) * piece, piece), piece), :]
+                own = part_of(side, c)
+                here = (c // PIECES) % 2 == o
 
                 @pl.when(head)
                 def _():
                     leaving[side, c] = own.astype(BF16)
 
-                @pl.when(jnp.logical_not(head))
+                @pl.when(jnp.logical_not(head) & jnp.logical_not(owner))
                 def _():
                     chain_copy(side, c).wait_recv()
-                    both = (own + arrived[side, c].astype(F32)).astype(BF16)
-
-                    @pl.when(owner)
-                    def _():
-                        operator[o, c] = both
-
-                    @pl.when(jnp.logical_not(owner))
-                    def _():
-                        leaving[side, c] = both
-
-                @pl.when(jnp.logical_not(owner))
+                    leaving[side, c] = (own + arrived[side, c].astype(F32)).astype(BF16)
+
+                @pl.when(owner & here)
+                def _():
+                    chain_copy(side, c).wait_recv()
+                    operator[o, c] = (own + arrived[side, c].astype(F32)).astype(BF16)
+                    swap_copy(c).wait_recv()
+                    cross_copy(side, c).wait_recv()
+                    operator[1 - o, c] = (given[c].astype(F32) + crossed[c].astype(F32)).astype(BF16)
+
+                @pl.when(jnp.logical_not(owner) & ((downstream[side] > 1) | here))
                 def _():
                     chain_copy(side, c).start()
 
-                @pl.when(owner & ((c // PIECES) % 2 != o))
-                def _():
-                    swap_copy(c).start()
+                @pl.when((downstream[side] == 1) & jnp.logical_not(here))
+                def _():
+                    cross_copy(side, c).start()
 
                 @pl.when(c == 0)
                 def _():
@@ -204,8 +224,10 @@
     inward = jnp.where(z == 0, 1, last - 1)
     rows_copy.wait_recv()
 
-    def place(w):
-        return every.at[x * local + w]
+    share = rows // PARTS
+
+    def place(w, part):
+        return every.at[x * local + w, pl.ds(part * share, share)]
 
     def own_copies(i):
         w = base + 2 * i + o
@@ -215,22 +237,21 @@
         for hop in range(1, width):
             for core in range(2):
                 copies.append((core, {"walk": lax.rem(x + hop, width), "orb": core}))
-        made = [
-            remote(result.at[i, core], place(w), own_sends.at[i, n], every_recv.at[x, w], where)
+        copies.append((1 - o, {"orb": 1 - o}))
+        return [
+            remote(
+                result.at[i, core, pl.ds(part * share, share)], place(w, part),
+                own_sends.at[i, n, part], every_recv.at[x, w, part], where,
+            )
+            for part in range(PARTS)
             for n, (core, where) in enumerate(copies)
         ]
-        made.append(
-            remote(result.at[i, 1 - o], place(w), own_sends.at[i, len(copies)], every_recv.at[x, w], {"orb": 1 - o})
-        )
-        return made
 
     def finish(i):
         @pl.when(at_end)
         def _():
             a = 2 * i + o
             w = base + a
-            for q in range(PIECES):
-                swap_arrival(a * PIECES + q).wait_recv()
 
             def tile(core, slot):
                 flat = operator[core, pl.ds(a * PIECES, PIECES)].reshape(packed, block)
@@ -280,12 +301,14 @@
     for hop in range(1, width):
         log_copy(hop).start()
 
-    def onward(w, hop_to):
-        return remote(place(w), place(w), next_send.at[w], every_recv.at[x, w], {"vec": hop_to})
-
-    def across(w, hop):
+    def onward(w, part, hop_to):
+        spot = place(w, part)
+        return remote(spot, spot, next_send.at[w, part], every_recv.at[x, w, part], {"vec": hop_to})
+
+    def across(w, part, hop):
+        spot = place(w, part)
         return remote(
-            place(w), place(w), across_send.at[hop - 1, w], every_recv.at[x, w], {"walk": lax.rem(x + hop, width)}
+            spot, spot, across_send.at[hop - 1, w, part], every_recv.at[x, w, part], {"walk": lax.rem(x + hop, width)}
         )
 
     near = jnp.where(z <= last - z, 0, 1)
@@ -298,29 +321,32 @@
 
     for i in range(mine):
         for side in (near, 1 - near):
-            for a in (2 * i, 2 * i + 1):
+            for part, a in [(part, a) for part in range(PARTS) for a in (2 * i, 2 * i + 1)]:
                 w, away, end, hop_to = route(side, a)
 
                 @pl.when(away > 0)
                 def _():
-                    onward(w, hop_to).wait_recv()
+                    onward(w, part, hop_to).wait_recv()
 
                     @pl.when(end > 0)
                     def _():
-                        onward(w, hop_to).start()
+                        onward(w, part, hop_to).start()
 
                     for hop in range(1, width):
-                        across(w, hop).start()
+                        across(w, part, hop).start()
 
                 @pl.when((away == 0) & (o != a % 2))
                 def _():
-                    onward(w, hop_to).wait_recv()
+                    onward(w, part, hop_to).wait_recv()
 
     for hop in range(1, width):
         other = lax.rem(x + hop, width)
         for w in range(local):
-            spot = every.at[other * local + w]
-            remote(spot, spot, across_send.at[hop - 1, w], every_recv.at[other, w], {"walk": other}).wait_recv()
+            for part in range(PARTS):
+                spot = every.at[other * local + w, pl.ds(part * share, share)]
+                remote(
+                    spot, spot, across_send.at[hop - 1, w, part], every_recv.at[other, w, part], {"walk": other}
+                ).wait_recv()
         remote(logs.at[other], logs.at[other], log_send.at[hop - 1], log_recv.at[other], {"walk": other}).wait_recv()
 
     for s in range(local):
@@ -365,10 +391,12 @@
             def _():
                 @pl.when(end > 0)
                 def _():
-                    onward(w, hop_to).wait_send()
+                    for part in range(PARTS):
+                        onward(w, part, hop_to).wait_send()
 
                 for hop in range(1, width):
-                    across(w, hop).wait_send()
+                    for part in range(PARTS):
+                        across(w, part, hop).wait_send()
 
 
 def per_device(depth, width, walkers, inv_intersection, trial, vectors, aux_field, log_weight, copy_list):
@@ -403,6 +431,8 @@
             pltpu.VMEM((local, packed, block), F32),
             pltpu.VMEM((2, chunks, piece, block), BF16),
             pltpu.VMEM((2, chunks, piece, block), BF16),
+            pltpu.VMEM((chunks, piece, block), BF16),
+            pltpu.VMEM((chunks, piece, block), BF16),
             pltpu.VMEM((2, chunks, piece, block), BF16),
             pltpu.VMEM((orbitals, orbitals), BF16),
             pltpu.VMEM((orbitals, electrons), BF16),
@@ -419,10 +449,11 @@
             dma((2,)),
             dma((chunks,)),
             dma((chunks,)),
-            dma((width, local)),
-            dma((mine, 2 * width + 1)),
-            dma((local,)),
-            dma((max(width - 1, 1), local)),
+            dma((chunks,)),
+            dma((width, local, PARTS)),
+            dma((mine, 2 * width + 1, PARTS)),
+            dma((local, PARTS)),
+            dma((max(width - 1, 1), local, PARTS)),
             dma((max(width - 1, 1),)),
             dma((width,)),
         ],

time: 56.4 us -> 54.6 us (0.968)
  Pallas kernels: 52.6 us -> 50.7 us
    pallas_call x1, Pallas kernels: 52.6 us -> 50.7 us  [per_device(): pl.pallas_call(functools.partial(kernel, depth, width), out_shape=(jax.Sh...]
where the time goes in v3:
time: 54.6 us; the launch traced here: 54.4 us
  Pallas kernels  50.7 us (93%)
  local copies, waits for them, and re-layouts  2.98 us (5%)
  between operations  0.64 us (1%)
    pallas_call x1, Pallas kernels, per_device(): pl.pallas_call(functools.partial(kernel, depth, width), out_shape=(jax.Sh...  50.7 us
    unnamed x2, local copies, waits for them, and re-layouts  2.98 us

profile of v3, /device:TPU:0, one launch (start us, length us, event | category | flops | bytes accessed | tf_op | source)
XLA Modules:
  0.0 54.4 jit_solution(928698976170805445)
XLA Ops:
  0.6 50.7 %shard_map.86 = (bf16[8,256,128]{2,1,0:T(8,128)(2,1)}, f32[8]{0:T(128)}) custom-call(bf16[8,256,128]{2,1,0:T(8,128)(2,1)} %walkers.1, bf16[8,128,128]{2,1,0:T(8,128)(2,1)} %inverse.1, bf16[512,128]{1,0:T(8,128)(2,1)} %trial.1, bf16[8,256,512]{2,1,0:T(8,128)(2,1)} %vectors.1, f32[8,8]{1,0:T(8,128)} %aux.1, f32[8]{0:T(128)} %log_weight.1, s32[8]{0:T(128)} %copy_list.1), custom_call_target="tpu_custom_call" | custom-call | tf_op jit(solution)/shard_map/pallas_call | solution.py:417
  51.4 1.9 %copy.11 = bf16[8,256,128]{2,1,0:T(8,128)(2,1)} copy(bf16[8,256,128]{2,1,0:T(8,128)(2,1)} %get-tuple-element.4) | data formatting | bytes 1048576
  53.3 1.1 %copy.12 = f32[8]{0:T(128)} copy(f32[8]{0:T(128)} %get-tuple-element.5) | data formatting | bytes 64
